TPU v7x, 32 devices: a whole 2x2x4 slice. The times are simulated.
32 devices in a mesh: fsdp: 8 (over z, core), chan: 4 (over y, x).
Axes of the slice: x: 2, y: 2, z: 4, core: 2. Of those that a mesh axis runs over, the one named last changes fastest.
Arguments:
- in_master: float32 [4096, 2, 4096], P(('fsdp', 'chan')), may hold values from -0.09375 to 0.09375
- in_moment: float32 [4096, 2, 4096], P(('fsdp', 'chan')), may hold values from -1.8 to 1.8
- in_velocity: float32 [4096, 2, 4096], P(('fsdp', 'chan')), may hold values from 0.05 to 1
- in_grad: bfloat16 [4096, 2, 4096], P(('fsdp', 'chan')), may hold values from -6 to 6
- out_master: float32 [4096, 4096], P(('fsdp', 'chan')), may hold values from -0.09375 to 0.09375
- out_moment: float32 [4096, 4096], P(('fsdp', 'chan')), may hold values from -1.8 to 1.8
- out_velocity: float32 [4096, 4096], P(('fsdp', 'chan')), may hold values from 0.001 to 1
- out_grad: bfloat16 [4096, 4096], P(('fsdp', 'chan')), may hold values from -6 to 6
- embed_table: bfloat16 [65536, 4096], P('fsdp', 'chan'), may hold values from -18 to 18
- tokens: int32 [4, 1024], P(None, 'fsdp'), may hold values from 0 to 65535, as said below
- conv_state: bfloat16 [1024, 3, 4096], P('fsdp', None, 'chan'), may hold values from -6 to 6
- ssm_state: float32 [1024, 16, 4096], P('fsdp', None, 'chan'), may hold values from -6 to 6
- conv_weight: float32 [4, 4096], P(None, 'chan'), may hold values from -3 to 3
- conv_bias: float32 [4096], P('chan'), may hold values from -3 to 3
- x_proj_w: bfloat16 [288, 4096], P(None, 'chan'), may hold values from -0.09375 to 0.09375
- dt_proj_w: bfloat16 [4096, 256], P('chan'), may hold values from -0.375 to 0.375
- dt_bias: float32 [4096], P('chan'), may hold values from -4.5 to -2
- a_log: float32 [16, 4096], P(None, 'chan'), may hold values from 0 to 2.77
- d_skip: float32 [4096], P('chan'), may hold values from 0.5 to 2
Outputs:
- in_master_new: float32 [4096, 2, 4096], P(('fsdp', 'chan'))
- out_master_new: float32 [4096, 4096], P(('fsdp', 'chan'))
- block_out: bfloat16 [4, 1024, 4096], P(None, 'fsdp', 'chan')
- conv_state_new: bfloat16 [1024, 3, 4096], P('fsdp', None, 'chan')
- ssm_state_new: float32 [1024, 16, 4096], P('fsdp', None, 'chan')
Inputs may be any that keep to these rules, and one draw needn't show every extreme that they name: Split the ids into 8 equal consecutive vocabulary blocks and the sequences into 8 equal consecutive replicas; of one replica's 4 x 128 tokens at most 128 lie in any one block, and some block holds exactly 128 of them.
All inputs are finite; a program needn't handle non-finite values.
Results may differ from a plain program's by a relative error of at most 0.012.
Values may be sent and summed in bfloat16 or wider, within the bound.
A program may use at most 192 MiB of HBM per device.

v0:
```python
import math
import jax
import jax.numpy as jnp
from jax import lax
from jax.sharding import PartitionSpec as P

RANK = 256
NSTATE = 16
learn_rate = 0.01
beta_first = 0.8
beta_second = 0.95
adam_eps = 1e-08
weight_decay = 0.1
bias_first = 1.0 - math.pow(0.8, 10)
bias_second = 1.0 - math.pow(0.95, 10)
norm_eps = 1e-06


def adam_update(master, moment, velocity, grad):
    gradient = grad.astype(jnp.float32)
    moment = beta_first * moment + (1.0 - beta_first) * gradient
    velocity = beta_second * velocity + (1.0 - beta_second) * gradient * gradient
    update = moment / bias_first / (jnp.sqrt(velocity / bias_second) + adam_eps)
    return master - learn_rate * (update + weight_decay * master)


def reorder_rows(block, groups, replicas):
    width = block.shape[1]
    shaped = block.reshape(groups, replicas, -1, width)
    return jnp.transpose(shaped, (1, 0, 2, 3)).reshape(-1, width)


def per_device(
    in_master,
    in_moment,
    in_velocity,
    in_grad,
    out_master,
    out_moment,
    out_velocity,
    out_grad,
    embed_table,
    tokens,
    conv_state,
    ssm_state,
    conv_weight,
    conv_bias,
    x_proj_w,
    dt_proj_w,
    dt_bias,
    a_log,
    d_skip,
):
    in_new = adam_update(in_master, in_moment, in_velocity, in_grad)
    out_new = adam_update(out_master, out_moment, out_velocity, out_grad)
    pieces = (
        in_new[:, 0, :].astype(jnp.bfloat16),
        in_new[:, 1, :].astype(jnp.bfloat16),
        out_new.astype(jnp.bfloat16),
    )
    groups = lax.axis_size("chan")
    replicas = lax.axis_size("fsdp")
    stacked = (
        lax.all_gather(pieces[0], "fsdp", axis=0, tiled=True),
        lax.all_gather(pieces[1], "fsdp", axis=0, tiled=True),
        lax.all_gather(pieces[2], "fsdp", axis=0, tiled=True),
    )
    spread = (
        lax.all_to_all(stacked[0], "chan", split_axis=1, concat_axis=0, tiled=True),
        lax.all_to_all(stacked[1], "chan", split_axis=1, concat_axis=0, tiled=True),
        lax.all_to_all(stacked[2], "chan", split_axis=1, concat_axis=0, tiled=True),
    )
    relay_x = reorder_rows(spread[0], groups, replicas)
    relay_z = reorder_rows(spread[1], groups, replicas)
    relay_out = reorder_rows(spread[2], groups, replicas)
    vocab_rows = embed_table.shape[0]
    every_token = lax.all_gather(tokens, "fsdp", axis=1, tiled=True)
    offset = every_token - lax.axis_index("fsdp") * vocab_rows
    inside = jnp.logical_and(offset >= 0, offset < vocab_rows)
    picked = jnp.take(embed_table, jnp.clip(offset, 0, vocab_rows - 1), axis=0)
    picked = jnp.where(inside[:, :, None], picked, jnp.zeros((), jnp.bfloat16))
    found = (
        lax.psum_scatter(picked, "fsdp", scatter_dimension=1, tiled=True)
        .astype(jnp.float32)
        .astype(jnp.bfloat16)
    )
    inputs = lax.all_gather(found, "chan", axis=2, tiled=True)
    steps, rows, width = inputs.shape
    flat = inputs.reshape(steps * rows, width).astype(jnp.float32)
    normed = (flat * lax.rsqrt(jnp.mean(flat * flat, axis=1, keepdims=True) + norm_eps)).astype(
        jnp.bfloat16
    )
    x_in = (
        jnp.dot(normed, relay_x, preferred_element_type=jnp.float32)
        .astype(jnp.bfloat16)
        .reshape(steps, rows, -1)
    )
    z_in = (
        jnp.dot(normed, relay_z, preferred_element_type=jnp.float32)
        .astype(jnp.bfloat16)
        .reshape(steps, rows, -1)
    )
    decay = -jnp.exp(a_log)
    contract_last = (((1,), (1,)), ((), ()))
    window_state = conv_state
    state = ssm_state
    gates = []
    for step in range(steps):
        window = jnp.concatenate([window_state, x_in[step][:, None, :]], axis=1)
        mixed_conv = jnp.sum(window.astype(jnp.float32) * conv_weight[None], axis=1) + conv_bias
        act = jax.nn.silu(mixed_conv).astype(jnp.bfloat16)
        partial_value = lax.dot_general(
            act, x_proj_w, contract_last, preferred_element_type=jnp.float32
        )
        dbc = lax.psum(partial_value, "chan")
        dt_low = dbc[:, :RANK].astype(jnp.bfloat16)
        b_mat = dbc[:, RANK : RANK + NSTATE]
        c_mat = dbc[:, RANK + NSTATE :]
        delta = jax.nn.softplus(
            lax.dot_general(dt_low, dt_proj_w, contract_last, preferred_element_type=jnp.float32)
            + dt_bias
        )
        act_real = act.astype(jnp.float32)
        state = (
            jnp.exp(delta[:, None, :] * decay[None]) * state
            + (delta * act_real)[:, None, :] * b_mat[:, :, None]
        )
        y_out = jnp.sum(c_mat[:, :, None] * state, axis=1) + d_skip * act_real
        gated = (y_out * jax.nn.silu(z_in[step].astype(jnp.float32))).astype(jnp.bfloat16)
        gates.append(gated)
        window_state = window[:, 1:, :]
    stacked_gates = jnp.stack(gates)
    terms = lax.dot_general(
        stacked_gates, relay_out, (((2,), (1,)), ((), ())), preferred_element_type=jnp.float32
    )
    mixed_all = lax.psum_scatter(
        terms.astype(jnp.bfloat16), "chan", scatter_dimension=2, tiled=True
    ).astype(jnp.float32)
    block_out = (found.astype(jnp.float32) + mixed_all).astype(jnp.bfloat16)
    return (in_new, out_new, block_out, window_state, state)


def solution(mesh):
    placed = (
        P(("fsdp", "chan"), None, None),
        P(("fsdp", "chan"), None, None),
        P(("fsdp", "chan"), None, None),
        P(("fsdp", "chan"), None, None),
        P(("fsdp", "chan"), None),
        P(("fsdp", "chan"), None),
        P(("fsdp", "chan"), None),
        P(("fsdp", "chan"), None),
        P("fsdp", "chan"),
        P(None, "fsdp"),
        P("fsdp", None, "chan"),
        P("fsdp", None, "chan"),
        P(None, "chan"),
        P("chan"),
        P(None, "chan"),
        P("chan", None),
        P("chan"),
        P(None, "chan"),
        P("chan"),
    )
    return jax.shard_map(
        per_device,
        mesh=mesh,
        in_specs=placed,
        out_specs=(
            P(("fsdp", "chan"), None, None),
            P(("fsdp", "chan"), None),
            P(None, "fsdp", "chan"),
            P("fsdp", None, "chan"),
            P("fsdp", None, "chan"),
        ),
        check_vma=False,
    )
```

profile of v0, /device:TPU:0, one launch (start us, length us, event | category | flops | bytes accessed | tf_op | source)
XLA Modules:
  0.0 634.5 jit_solution(9839498305490577094)
XLA Ops:
  7.2 3.0 copy.58
  10.3 1.8 copy.56
  12.1 2.3 copy.55
  14.3 2.9 copy.54
  17.2 5.8 fusion.65
  23.1 7.2 %copy.53 = f32[128,2,4096]{0,2,1:T(8,128)} copy(f32[128,2,4096]{2,1,0:T(2,128)} %param.19) | data formatting | bytes 8388608 | tf_op args[0]
  30.3 7.4 %copy.51 = f32[128,2,4096]{0,2,1:T(8,128)} copy(f32[128,2,4096]{2,1,0:T(2,128)} %param.21) | data formatting | bytes 8388608 | tf_op args[2]
  37.7 6.2 copy.50
  43.9 7.3 %copy.49 = f32[128,2,4096]{0,2,1:T(8,128)} copy(f32[128,2,4096]{2,1,0:T(2,128)} %param.20) | data formatting | bytes 8388608 | tf_op args[1]
  51.2 8.4 %fusion.63 = (bf16[128,2,4096]{0,2,1:T(8,128)(2,1)S(1)}, f32[128,2,4096]{0,2,1:T(8,128)}) fusion(f32[128,2,4096]{0,2,1:T(8,128)} %copy.53, f32[128,2,4096]{0,2,1:T(8,128)} %copy.51, bf16[128,2,4096]{0,2,1:T(8,128)(2,1)} %copy.50, f32[128,2,4096]{0,2,1:T(8,128)} %copy.49), kind=kLoop, calls=%fused_computation.141 | loop fusion | flops 17825792 | bytes 20971520 | tf_op jit(solution)/shard_map/convert.5
  59.7 1.4 fusion.67
  61.2 0.7 all-gather.11.cloned.1.call-update
  61.9 25.0 %all_gather.15 = s32[4,1024]{1,0:T(4,128)S(1)} all-gather(s32[4,128]{1,0:T(4,128)S(1)} %copy-done.24), channel_id=1, replica_groups=mesh['fsdp'=8,'chan'=4] {'fsdp'}, dimensions={1}, use_global_device_ids=true | all-gather | bytes 18432 | tf_op jit(solution)/shard_map/all_gather | solution.py:77
  87.0 28.8 %gather_fusion = bf16[4096,1024]{1,0:T(8,128)(2,1)} fusion(bf16[8192,1024]{1,0:T(8,128)(2,1)} %param.27, s32[4096]{0:T(1024)S(1)} %bitcast_clamp_fusion), kind=kCustom, calls=%fused_computation | custom fusion | bytes 16793600 | tf_op jit(solution)/shard_map/jit(_take)/gather | solution.py:80
  115.8 7.9 %select_select_fusion = bf16[4,1024,1024]{2,1,0:T(8,128)(2,1)} fusion(bf16[4,1024,1024]{2,1,0:T(8,128)(2,1)} %bitcast.69, pred[4,1024]{1,0:T(4,128)(4,1)S(1)} %get-tuple-element.53, pred[4,1024]{1,0:T(4,128)(4,1)S(1)} %get-tuple-element.52), kind=kLoop, calls=%fused_computation.13 | loop fusion | flops 8388608 | bytes 16785408 | tf_op jit(solution)/shard_map/jit(_where)/select_n | solution.py:81
  123.7 5.6 all-to-all-start.2
  129.4 62.1 %all-gather.13.cloned.1.call-done = bf16[1024,1,4096]{0,2,1:T(8,128)(2,1)} async-done(((bf16[128,1,4096]{0,2,1:T(8,128)(2,1)}), bf16[1024,1,4096]{0,2,1:T(8,128)(2,1)}) %all-gather.13.cloned.1.call-update) | async-done | bytes 8388624 | tf_op jit(solution)/shard_map/all_gather | solution.py:65
  191.4 31.0 %all-to-all-done.2 = bf16[1024,4,1024]{0,2,1:T(8,128)(2,1)} async-done(((bf16[1024,4,1024]{0,2,1:T(8,128)(2,1)}), bf16[1024,4,1024]{0,2,1:T(8,128)(2,1)}, u32[]{:S(2)}, u32[]{:S(2)}) %all-to-all-start.2) | async-done | bytes 8388640 | tf_op jit(solution)/shard_map/all_to_all | solution.py:71
  222.5 5.7 all-to-all-start.1
  228.2 46.1 %all-gather.11.cloned.1.call-done = bf16[1024,1,4096]{0,2,1:T(8,128)(2,1)} async-done(((bf16[128,1,4096]{0,2,1:T(8,128)(2,1)}), bf16[1024,1,4096]{0,2,1:T(8,128)(2,1)}) %all-gather.11.cloned.1.call-update) | async-done | bytes 8388624 | tf_op jit(solution)/shard_map/all_gather | solution.py:64
  274.3 46.1 %all-to-all-done.1 = bf16[1024,4,1024]{0,2,1:T(8,128)(2,1)} async-done(((bf16[1024,4,1024]{0,2,1:T(8,128)(2,1)}), bf16[1024,4,1024]{0,2,1:T(8,128)(2,1)}, u32[]{:S(2)}, u32[]{:S(2)}) %all-to-all-start.1) | async-done | bytes 8388640 | tf_op jit(solution)/shard_map/all_to_all | solution.py:70
  320.4 5.8 all-to-all-start
  326.3 38.5 %reduce-scatter.3.cloned.1.call-done = bf16[4,128,1024]{2,1,0:T(8,128)(2,1)} async-done(((bf16[4,1024,1024]{2,1,0:T(8,128)(2,1)}), bf16[4,128,1024]{2,1,0:T(8,128)(2,1)}) %reduce-scatter.3.cloned.1.call-update) | async-done | bytes 1048592 | tf_op jit(solution)/shard_map/reduce_scatter | solution.py:83
  365.3 11.6 %copy.69 = bf16[4,1024,1024]{2,1,0:T(8,128)(2,1)} copy(bf16[4,1024,1024]{1,2,0:T(8,128)(2,1)} %bitcast.19) | data formatting | bytes 16777216 | tf_op jit(solution)/shard_map/all_to_all | solution.py:71
  376.9 8.2 %copy.70 = bf16[8,4,128,1024]{3,2,1,0:T(8,128)(2,1)} copy(bf16[8,4,128,1024]{3,2,0,1:T(8,128)(2,1)} %bitcast.70) | data formatting | bytes 16777216 | tf_op jit(solution)/shard_map/transpose | solution.py:30
  385.1 8.9 %copy.75 = bf16[512,8,8,128]{3,2,1,0:T(8,128)(2,1)} copy(bf16[512,8,8,128]{3,1,2,0:T(8,128)(2,1)} %bitcast.38) | data formatting | bytes 16777216
  394.1 12.2 %copy.62 = bf16[4,8,128,1024]{3,2,0,1:T(8,128)(2,1)} copy(bf16[4,8,128,1024]{2,1,3,0:T(8,128)(2,1)} %bitcast.71) | data formatting | bytes 16777216 | tf_op jit(solution)/shard_map/reshape | solution.py:29
  406.2 23.1 %all-to-all-done = bf16[1024,4,1024]{0,2,1:T(8,128)(2,1)} async-done(((bf16[1024,4,1024]{0,2,1:T(8,128)(2,1)}), bf16[1024,4,1024]{0,2,1:T(8,128)(2,1)}, u32[]{:S(2)}, u32[]{:S(2)}) %all-to-all-start) | async-done | bytes 8388640 | tf_op jit(solution)/shard_map/all_to_all | solution.py:69
  429.3 9.2 %copy.74 = bf16[512,8,8,128]{3,2,1,0:T(8,128)(2,1)} copy(bf16[512,8,8,128]{3,1,2,0:T(8,128)(2,1)} %bitcast.32) | data formatting | bytes 16777216
  438.6 12.3 %copy.59 = bf16[4,8,128,1024]{3,2,0,1:T(8,128)(2,1)} copy(bf16[4,8,128,1024]{2,1,3,0:T(8,128)(2,1)} %bitcast.72) | data formatting | bytes 16777216 | tf_op jit(solution)/shard_map/reshape | solution.py:29
  450.9 6.1 all-gather.7.cloned.1.call-done
  457.0 3.2 fusion
  460.4 1.5 fusion.1
  461.9 3.4 copy-done.2
  465.3 4.5 convolution_convert_fusion.2
  470.6 1.4 multiply_reduce_fusion.7
  473.3 1.0 fusion.75
  474.3 1.0 fusion.74
  475.3 1.0 fusion.73
  476.2 1.0 fusion.72
  477.5 10.2 %convolution_convert_fusion.1 = bf16[512,1024]{1,0:T(8,128)(2,1)} fusion(bf16[512,4096]{1,0:T(8,128)(2,1)} %bitcast.82, bf16[4096,1024]{1,0:T(8,128)(2,1)} %bitcast.79), kind=kOutput, calls=%fused_computation.48 | convolution fusion | flops 4295491584 | bytes 13631488 | tf_op jit(solution)/shard_map/dot_general | solution.py:99
  487.7 35.9 %all-reduce.3.cloned.1.call-done = (f32[128,288]{0,1:T(8,128)}, f32[128,288]{0,1:T(8,128)}, f32[128,288]{0,1:T(8,128)}, f32[128,288]{0,1:T(8,128)}) async-done(((f32[128,288]{0,1:T(8,128)}, f32[128,288]{0,1:T(8,128)}, f32[128,288]{0,1:T(8,128)}, f32[128,288]{0,1:T(8,128)}), (f32[128,288]{0,1:T(8,128)}, f32[128,288]{0,1:T(8,128)}, f32[128,288]{0,1:T(8,128)}, ...) | async-done | bytes 589840 | tf_op jit(solution)/shard_map/psum | solution.py:115
  523.6 1.4 fusion.68
  525.0 2.4 convert_multiply_fusion.15
  527.5 2.5 convert_multiply_fusion.9
  530.0 2.5 convert_multiply_fusion.12
  532.6 1.3 fusion.70
  533.9 1.5 convert_multiply_fusion.6
  535.4 1.4 copy.63
  536.8 1.4 copy.64
  538.3 1.4 copy.61
  539.7 1.4 copy.66
  541.1 1.4 copy.65
  542.5 0.7 copy.60
  543.2 1.4 copy.68
  544.6 1.4 copy.67
  546.1 17.0 %multiply_reduce_fusion.2 = (f32[128,1024]{1,0:T(8,128)S(1)}, f32[128,1024]{1,0:T(8,128)S(1)}, f32[128,1024]{1,0:T(8,128)S(1)}, f32[128,1024]{1,0:T(8,128)S(1)}, f32[128,16,1024]{2,1,0:T(8,128)}) fusion(f32[128,16]{1,0:T(8,128)} %copy.63, f32[128,16]{1,0:T(8,128)} %copy.64, f32[128,1024]{1,0:T(8,128)} %get-tuple-element.58, f32[128,16]{1,0:T(8,128)} %copy.61, ...), kind=kLoop, calls=%fused_computation.9 | loop fusion | flops 49807360 | bytes 23199744 | tf_op jit(solution)/shard_map/reduce_sum | solution.py:128
  563.2 1.5 fusion.60
  564.7 7.1 %convolution_convert_fusion = bf16[4,128,4096]{2,1,0:T(8,128)(2,1)} fusion(bf16[4096,1024,1]{1,0,2:T(8,128)(2,1)S(1)} %bitcast.75, bf16[1,128,1024]{2,1,0:T(8,128)(2,1)S(1)} %get-tuple-element.37, bf16[1,128,1024]{2,1,0:T(8,128)(2,1)S(1)} %get-tuple-element.38, bf16[1,128,1024]{2,1,0:T(8,128)(2,1)} %get-tuple-element.39, ...), kind=kOutput, calls=%fused_computation.15 | convolution fusion | flops 4298637312 | bytes 13631488 | tf_op jit(solution)/shard_map/dot_general | solution.py:133
  571.8 7.2 %copy.71 = f32[128,2,4096]{2,1,0:T(2,128)} copy(f32[128,2,4096]{0,2,1:T(8,128)} %get-tuple-element.29) | data formatting | bytes 8388608
  579.0 1.8 copy.72
  580.9 1.9 fusion.29
  582.7 41.8 %reduce-scatter.5.cloned.1.call-done = bf16[4,128,1024]{2,1,0:T(8,128)(2,1)} async-done(((bf16[4,128,4096]{2,1,0:T(8,128)(2,1)}), bf16[4,128,1024]{2,1,0:T(8,128)(2,1)}) %reduce-scatter.5.cloned.1.call-update) | async-done | bytes 1048592 | tf_op jit(solution)/shard_map/reduce_scatter | solution.py:136
  624.5 2.9 add_convert_fusion
  (78 shorter events, 3.4 us)
Async XLA Ops:
  7.2 466.1 %copy-start = (bf16[288,1024]{1,0:T(8,128)(2,1)S(1)}, bf16[288,1024]{1,0:T(8,128)(2,1)}, u32[]{:S(2)}) copy-start(bf16[288,1024]{1,0:T(8,128)(2,1)} %param.33) | copy-start | bytes 1769476
  7.2 3.1 copy-start.16
  7.2 116.5 %all-gather.9.cloned.1.call-start = ((), (), s32[]{:S(2)}) async-start(), calls=%async_computation.7 | async-start | bytes 9437184 | tf_op jit(solution)/shard_map/all_gather | solution.py:66
  23.1 168.3 %all-gather.13.cloned.1.call-start = ((), (), s32[]{:S(2)}) async-start(), calls=%async_computation.10 | async-start | bytes 9437184 | tf_op jit(solution)/shard_map/all_gather | solution.py:65
  59.7 2.3 copy-start.24
  61.1 213.2 %all-gather.11.cloned.1.call-start = ((), (), s32[]{:S(2)}) async-start(), calls=%async_computation.9 | async-start | bytes 9437184 | tf_op jit(solution)/shard_map/all_gather | solution.py:64
  61.9 302.9 %reduce-scatter.3.cloned.1.call-start = ((), (), s32[]{:S(2)}) async-start(), calls=%async_computation.5 | async-start | bytes 9437184 | tf_op jit(solution)/shard_map/reduce_scatter | solution.py:83
  123.7 98.7 %all-to-all-start.2 = ((bf16[1024,4,1024]{0,2,1:T(8,128)(2,1)}), bf16[1024,4,1024]{0,2,1:T(8,128)(2,1)}, u32[]{:S(2)}, u32[]{:S(2)}) async-start(bf16[1024,4,1024]{0,2,1:T(8,128)(2,1)} %bitcast.77), calls=%async_computation.3 | async-start | bytes 16777216 | tf_op jit(solution)/shard_map/all_to_all | solution.py:71
  222.5 97.9 %all-to-all-start.1 = ((bf16[1024,4,1024]{0,2,1:T(8,128)(2,1)}), bf16[1024,4,1024]{0,2,1:T(8,128)(2,1)}, u32[]{:S(2)}, u32[]{:S(2)}) async-start(bf16[1024,4,1024]{0,2,1:T(8,128)(2,1)} %bitcast.78), calls=%async_computation.2 | async-start | bytes 16777216 | tf_op jit(solution)/shard_map/all_to_all | solution.py:70
  320.4 44.9 %copy-start.20 = (f32[16,1024]{1,0:T(8,128)S(1)}, f32[16,1024]{1,0:T(8,128)}, u32[]{:S(2)}) copy-start(f32[16,1024]{1,0:T(8,128)} %param.36) | copy-start | bytes 196612
  320.4 108.9 %all-to-all-start = ((bf16[1024,4,1024]{0,2,1:T(8,128)(2,1)}), bf16[1024,4,1024]{0,2,1:T(8,128)(2,1)}, u32[]{:S(2)}, u32[]{:S(2)}) async-start(bf16[1024,4,1024]{0,2,1:T(8,128)(2,1)} %bitcast.76), calls=%async_computation.1 | async-start | bytes 16777216 | tf_op jit(solution)/shard_map/all_to_all | solution.py:69
  326.3 130.7 %all-gather.7.cloned.1.call-start = ((), (), s32[]{:S(2)}) async-start(), calls=%async_computation.6 | async-start | bytes 5242880 | tf_op jit(solution)/shard_map/all_gather | solution.py:87
  364.8 158.8 %all-reduce.3.cloned.1.call-start = ((), (), s32[]{:S(2)}) async-start(), calls=%async_computation.11 | async-start | bytes 1179648 | tf_op jit(solution)/shard_map/psum | solution.py:115
  457.0 3.4 copy-start.1
  460.4 4.9 copy-start.2
  461.9 7.9 %copy-start.6 = (bf16[4,128,4096]{2,1,0:T(8,128)(2,1)}, bf16[4,128,4096]{2,1,0:T(8,128)(2,1)S(1)}, u32[]{:S(2)}) copy-start(bf16[4,128,4096]{2,1,0:T(8,128)(2,1)S(1)} %fusion.1) | copy-start | bytes 12582916
  465.3 4.6 copy-start.14
  469.9 0.7 copy-start.21
  470.0 2.0 copy-start.15
  470.1 1.9 copy-start.22
  470.2 2.4 copy-start.4
  472.6 0.7 copy-start.11
  472.6 4.9 copy-start.7
  472.6 4.9 copy-start.9
  477.2 147.3 %reduce-scatter.5.cloned.1.call-start = ((), (), s32[]{:S(2)}) async-start(), calls=%async_computation.8 | async-start | bytes 5242880 | tf_op jit(solution)/shard_map/reduce_scatter | solution.py:136
  477.5 47.5 %copy-start.3 = (bf16[1024,256]{1,0:T(8,128)(2,1)S(1)}, bf16[1024,256]{1,0:T(8,128)(2,1)}, u32[]{:S(2)}) copy-start(bf16[1024,256]{1,0:T(8,128)(2,1)} %param.34) | copy-start | bytes 1572868
  477.5 47.5 %copy-start.19 = (f32[1024]{0:T(1024)S(1)}, f32[1024]{0:T(1024)}, u32[]{:S(2)}) copy-start(f32[1024]{0:T(1024)} %param.35) | copy-start | bytes 12292
  523.6 8.9 %copy-start.18 = (f32[128,288]{0,1:T(8,128)S(1)}, f32[128,288]{0,1:T(8,128)}, u32[]{:S(2)}) copy-start(f32[128,288]{0,1:T(8,128)} %get-tuple-element.22) | copy-start | bytes 442372
  523.6 10.3 %copy-start.12 = (bf16[128,1024]{1,0:T(8,128)(2,1)S(1)}, bf16[128,1024]{1,0:T(8,128)(2,1)}, u32[]{:S(2)}) copy-start(bf16[128,1024]{1,0:T(8,128)(2,1)} %copy-done.11) | copy-start | bytes 786436
  546.1 18.6 %slice-start = ((s8[8388608]{0:T(1024)(128)(4,1)}), s8[4194304]{0:T(1024)(128)(4,1)S(1)}, s32[]{:S(2)}) async-start(s8[8388608]{0:T(1024)(128)(4,1)} %bitcast.73), calls=%async_computation.12 | async-start | bytes 8388608
  546.1 17.0 %copy-start.8 = (bf16[128,1024]{1,0:T(8,128)(2,1)S(1)}, bf16[128,1024]{1,0:T(8,128)(2,1)}, u32[]{:S(2)}) copy-start(bf16[128,1024]{1,0:T(8,128)(2,1)} %copy-done.7) | copy-start | bytes 786436
  546.1 17.0 %copy-start.10 = (bf16[128,1024]{1,0:T(8,128)(2,1)S(1)}, bf16[128,1024]{1,0:T(8,128)(2,1)}, u32[]{:S(2)}) copy-start(bf16[128,1024]{1,0:T(8,128)(2,1)} %copy-done.9) | copy-start | bytes 786436
  546.1 17.1 %copy-start.13 = (bf16[128,1024]{1,0:T(8,128)(2,1)S(1)}, bf16[128,1024]{1,0:T(8,128)(2,1)}, u32[]{:S(2)}) copy-start(bf16[128,1024]{1,0:T(8,128)(2,1)} %copy-done.11) | copy-start | bytes 786436
  546.1 17.1 %copy-start.17 = (bf16[512,1024]{1,0:T(8,128)(2,1)S(1)}, bf16[512,1024]{1,0:T(8,128)(2,1)}, u32[]{:S(2)}) copy-start(bf16[512,1024]{1,0:T(8,128)(2,1)} %convolution_convert_fusion.1) | copy-start | bytes 3145732
  546.1 17.1 %copy-start.23 = (f32[1024]{0:T(1024)S(1)}, f32[1024]{0:T(1024)}, u32[]{:S(2)}) copy-start(f32[1024]{0:T(1024)} %param.37) | copy-start | bytes 12292
  546.1 18.6 %slice-start.1 = ((s8[8388608]{0:T(1024)(128)(4,1)}), s8[4194304]{0:T(1024)(128)(4,1)S(1)}, s32[]{:S(2)}) async-start(s8[8388608]{0:T(1024)(128)(4,1)} %bitcast.73), calls=%async_computation.13 | async-start | bytes 8388608
  579.0 1.8 copy-start.5
Sparse Core Ops, SparseCore 0:
  23.2 85.2 all-gather.8
  110.7 80.6 all-gather.12
  193.6 80.6 all-gather.10
  277.0 87.6 reduce-scatter.2
  366.4 90.4 all-gather.6
  477.4 46.2 all-reduce.2
  571.9 52.5 reduce-scatter.4
where the time goes:
time: 645 us; the launch traced here: 635 us
  waiting for transfers between devices  332 us (51%)
  local copies, waits for them, and re-layouts  158 us (24%)
  other arithmetic  52.4 us (8%)
  matrix products  34.7 us (5%)
  blocking collectives  25 us (4%)
  starting transfers between devices  18.1 us (3%)
  between operations  14.8 us (2%)
    unnamed x66, local copies, waits for them, and re-layouts  70 us
    all_gather x1, waiting for transfers between devices, per_device(): lax.all_gather(pieces[1], 'fsdp', axis=0, tiled=True)  62.1 us
    all_gather x1, waiting for transfers between devices, per_device(): lax.all_gather(pieces[0], 'fsdp', axis=0, tiled=True)  46.1 us
    all_to_all x1, waiting for transfers between devices, per_device(): lax.all_to_all(stacked[1], 'chan', split_axis=1, concat_axis=0, tiled=True)  46.1 us
    reduce_scatter x1, waiting for transfers between devices, per_device(): lax.psum_scatter(terms.astype(jnp.bfloat16), 'chan', scatter_dimension=2,...  41.8 us
    reduce_scatter x1, waiting for transfers between devices, per_device(): lax.psum_scatter(picked, 'fsdp', scatter_dimension=1, tiled=True)  38.5 us
    psum x1, waiting for transfers between devices, per_device(): dbc = lax.psum(partial_value, 'chan')  35.9 us
    all_to_all x1, waiting for transfers between devices, per_device(): lax.all_to_all(stacked[2], 'chan', split_axis=1, concat_axis=0, tiled=True)  31 us
  transfers between devices with their start and end apart: 10, of which 9 were waited for; matrix products, arithmetic and copies ran while one was open for 25% of the time, Pallas kernels for 0%

commit v1 on v0

--- a/solution.py
+++ b/solution.py
@@ -68,7 +68,12 @@
     spread = (
         lax.all_to_all(stacked[0], "chan", split_axis=1, concat_axis=0, tiled=True),
         lax.all_to_all(stacked[1], "chan", split_axis=1, concat_axis=0, tiled=True),
-        lax.all_to_all(stacked[2], "chan", split_axis=1, concat_axis=0, tiled=True),
+        jnp.concatenate(
+            lax.all_to_all(
+                jnp.stack(jnp.split(stacked[2], lax.axis_size("chan"), axis=1)), "chan", 0, 0
+            ),
+            axis=0,
+        ),
     )
     relay_x = reorder_rows(spread[0], groups, replicas)
     relay_z = reorder_rows(spread[1], groups, replicas)

time: 645 us -> 614 us (0.952); the launches traced: 635 us -> 612 us
  local copies, waits for them, and re-layouts: 158 us -> 127 us
  waiting for transfers between devices: 332 us -> 349 us
  blocking collectives: 25 us -> 16 us
    unnamed x66 -> x41, local copies, waits for them, and re-layouts: 70 us -> 56.4 us
    another operation x0 -> x2, local copies, waits for them, and re-layouts: none -> 13 us  [the longest x1 8.58 us: reorder_rows(): shaped = block.reshape(groups, replicas, -1, width)]
    all_to_all x1 -> x0, local copies, waits for them, and re-layouts: 11.6 us -> none  [per_device(): lax.all_to_all(stacked[2], 'chan', split_axis=1, concat_axis=0, tiled=True)]
    all_to_all x1, waiting for transfers between devices: 23.1 us -> 33 us  [per_device(): lax.all_to_all(stacked[0], 'chan', split_axis=1, concat_axis=0, tiled=True)]
    all_gather x1, blocking collectives: 25 us -> 16 us  [per_device(): every_token = lax.all_gather(tokens, 'fsdp', axis=1, tiled=True)]
    transpose x1 -> x0, local copies, waits for them, and re-layouts: 8.25 us -> none  [reorder_rows(): return jnp.transpose(shaped, (1, 0, 2, 3)).reshape(-1, width)]
where the time goes in v1:
time: 614 us; the launch traced here: 612 us
  waiting for transfers between devices  349 us (57%)
  local copies, waits for them, and re-layouts  127 us (21%)
  other arithmetic  53.9 us (9%)
  matrix products  33.7 us (5%)
  starting transfers between devices  17.8 us (3%)
  blocking collectives  16 us (3%)
  between operations  14.5 us (2%)
    all_gather x1, waiting for transfers between devices, per_device(): lax.all_gather(pieces[1], 'fsdp', axis=0, tiled=True)  64.1 us
    unnamed x41, local copies, waits for them, and re-layouts  56.4 us
    all_gather x1, waiting for transfers between devices, per_device(): lax.all_gather(pieces[0], 'fsdp', axis=0, tiled=True)  48.1 us
    reduce_scatter x1, waiting for transfers between devices, per_device(): lax.psum_scatter(terms.astype(jnp.bfloat16), 'chan', scatter_dimension=2,...  44.5 us
    all_to_all x1, waiting for transfers between devices, per_device(): lax.all_to_all(stacked[1], 'chan', split_axis=1, concat_axis=0, tiled=True)  44.2 us
    reduce_scatter x1, waiting for transfers between devices, per_device(): lax.psum_scatter(picked, 'fsdp', scatter_dimension=1, tiled=True)  39.8 us
    psum x1, waiting for transfers between devices, per_device(): dbc = lax.psum(partial_value, 'chan')  35.9 us
    all_to_all x1, waiting for transfers between devices, per_device(): lax.all_to_all(stacked[0], 'chan', split_axis=1, concat_axis=0, tiled=True)  33 us
  transfers between devices with their start and end apart: 10, of which 9 were waited for; matrix products, arithmetic and copies ran while one was open for 25% of the time, Pallas kernels for 0%

profile of v1, /device:TPU:0, one launch (start us, length us, event | category | flops | bytes accessed | tf_op | source)
XLA Modules:
  0.0 611.9 jit_solution(9844813553168000914)
XLA Ops:
  7.2 6.5 %fusion.65 = (bf16[128,4096]{1,0:T(8,128)(2,1)}, f32[128,4096]{1,0:T(8,128)}) fusion(f32[128,4096]{1,0:T(8,128)} %param.23, f32[128,4096]{1,0:T(8,128)} %param.25, bf16[128,4096]{1,0:T(8,128)(2,1)} %param.26, f32[128,4096]{1,0:T(8,128)} %param.24), kind=kLoop, calls=%fused_computation.147 | loop fusion | flops 8912896 | bytes 10485760 | tf_op jit(solution)/shard_map/convert_element_type | solution.py:59
  13.8 7.2 %copy.37 = f32[128,2,4096]{0,2,1:T(8,128)} copy(f32[128,2,4096]{2,1,0:T(2,128)} %param.19) | data formatting | bytes 8388608 | tf_op args[0]
  21.1 7.4 %copy.35 = f32[128,2,4096]{0,2,1:T(8,128)} copy(f32[128,2,4096]{2,1,0:T(2,128)} %param.21) | data formatting | bytes 8388608 | tf_op args[2]
  28.5 4.9 copy.34
  33.4 7.3 %copy.33 = f32[128,2,4096]{0,2,1:T(8,128)} copy(f32[128,2,4096]{2,1,0:T(2,128)} %param.20) | data formatting | bytes 8388608 | tf_op args[1]
  40.7 7.9 %fusion.63 = (bf16[128,2,4096]{0,2,1:T(8,128)(2,1)S(1)}, f32[128,2,4096]{0,2,1:T(8,128)}) fusion(f32[128,2,4096]{0,2,1:T(8,128)} %copy.37, f32[128,2,4096]{0,2,1:T(8,128)} %copy.35, bf16[128,2,4096]{0,2,1:T(8,128)(2,1)S(1)} %copy.34, f32[128,2,4096]{0,2,1:T(8,128)} %copy.33), kind=kLoop, calls=%fused_computation.146 | loop fusion | flops 17825792 | bytes 20971520 | tf_op jit(solution)/shard_map/convert.5
  48.6 1.5 fusion.67
  50.1 0.7 all-gather.11.cloned.1.call-update
  50.9 16.0 %all_gather.15 = s32[4,1024]{1,0:T(4,128)S(1)} all-gather(s32[4,128]{1,0:T(4,128)S(1)} %copy-done.14), channel_id=1, replica_groups=mesh['fsdp'=8,'chan'=4] {'fsdp'}, dimensions={1}, use_global_device_ids=true | all-gather | bytes 18432 | tf_op jit(solution)/shard_map/all_gather | solution.py:82
  66.9 28.9 %gather_fusion = bf16[4096,1024]{1,0:T(8,128)(2,1)} fusion(bf16[8192,1024]{1,0:T(8,128)(2,1)} %param.27, s32[4096]{0:T(1024)S(1)} %bitcast_clamp_fusion), kind=kCustom, calls=%fused_computation | custom fusion | bytes 16793600 | tf_op jit(solution)/shard_map/jit(_take)/gather | solution.py:85
  95.8 7.6 %select_select_fusion = bf16[4,1024,1024]{2,1,0:T(8,128)(2,1)} fusion(bf16[4,1024,1024]{2,1,0:T(8,128)(2,1)} %bitcast.75, pred[4,1024]{1,0:T(4,128)(4,1)S(1)} %get-tuple-element.52, pred[4,1024]{1,0:T(4,128)(4,1)S(1)} %get-tuple-element.51), kind=kLoop, calls=%fused_computation.14 | loop fusion | flops 8388608 | bytes 16785408 | tf_op jit(solution)/shard_map/jit(_where)/select_n | solution.py:86
  103.4 4.4 slice_bitcast_fusion.3
  107.8 3.9 pad_maximum_fusion
  111.7 5.6 all-to-all-start.2
  117.4 64.1 %all-gather.13.cloned.1.call-done = bf16[1024,1,4096]{0,2,1:T(8,128)(2,1)} async-done(((bf16[128,1,4096]{0,2,1:T(8,128)(2,1)}), bf16[1024,1,4096]{0,2,1:T(8,128)(2,1)}) %all-gather.13.cloned.1.call-update) | async-done | bytes 8388624 | tf_op jit(solution)/shard_map/all_gather | solution.py:65
  181.4 29.1 %all-to-all-done.2 = bf16[4,1024,1024]{2,1,0:T(8,128)(2,1)} async-done(((bf16[4,1024,1024]{2,1,0:T(8,128)(2,1)}), bf16[4,1024,1024]{2,1,0:T(8,128)(2,1)}, u32[]{:S(2)}, u32[]{:S(2)}) %all-to-all-start.2) | async-done | bytes 8388640 | tf_op jit(solution)/shard_map/all_to_all | solution.py:72
  210.5 5.7 all-to-all-start.1
  216.2 48.1 %all-gather.11.cloned.1.call-done = bf16[1024,1,4096]{0,2,1:T(8,128)(2,1)} async-done(((bf16[128,1,4096]{0,2,1:T(8,128)(2,1)}), bf16[1024,1,4096]{0,2,1:T(8,128)(2,1)}) %all-gather.11.cloned.1.call-update) | async-done | bytes 8388624 | tf_op jit(solution)/shard_map/all_gather | solution.py:64
  264.3 44.2 %all-to-all-done.1 = bf16[1024,4,1024]{0,2,1:T(8,128)(2,1)} async-done(((bf16[1024,4,1024]{0,2,1:T(8,128)(2,1)}), bf16[1024,4,1024]{0,2,1:T(8,128)(2,1)}, u32[]{:S(2)}, u32[]{:S(2)}) %all-to-all-start.1) | async-done | bytes 8388640 | tf_op jit(solution)/shard_map/all_to_all | solution.py:70
  308.5 5.8 all-to-all-start
  314.4 39.8 %reduce-scatter.3.cloned.1.call-done = bf16[4,128,1024]{2,1,0:T(8,128)(2,1)} async-done(((bf16[4,1024,1024]{2,1,0:T(8,128)(2,1)}), bf16[4,128,1024]{2,1,0:T(8,128)(2,1)}) %reduce-scatter.3.cloned.1.call-update) | async-done | bytes 1048592 | tf_op jit(solution)/shard_map/reduce_scatter | solution.py:88
  354.2 0.2 all-reduce.3.cloned.1.call-start
  354.5 8.6 %copy.48 = bf16[4,8,128,1024]{3,2,0,1:T(8,128)(2,1)} copy(bf16[4,8,128,1024]{3,2,1,0:T(8,128)(2,1)} %bitcast.22) | data formatting | bytes 16777216 | tf_op jit(solution)/shard_map/reshape;reshape | solution.py:29
  363.1 9.2 %copy.52 = bf16[512,8,8,128]{3,2,1,0:T(8,128)(2,1)} copy(bf16[512,8,8,128]{3,1,2,0:T(8,128)(2,1)} %bitcast.40) | data formatting | bytes 16777216
  372.2 12.3 %copy.41 = bf16[4,8,128,1024]{3,2,0,1:T(8,128)(2,1)} copy(bf16[4,8,128,1024]{2,1,3,0:T(8,128)(2,1)} %bitcast.76) | data formatting | bytes 16777216 | tf_op jit(solution)/shard_map/reshape | solution.py:29
  384.5 33.0 %all-to-all-done = bf16[1024,4,1024]{0,2,1:T(8,128)(2,1)} async-done(((bf16[1024,4,1024]{0,2,1:T(8,128)(2,1)}), bf16[1024,4,1024]{0,2,1:T(8,128)(2,1)}, u32[]{:S(2)}, u32[]{:S(2)}) %all-to-all-start) | async-done | bytes 8388640 | tf_op jit(solution)/shard_map/all_to_all | solution.py:69
  417.5 9.0 %copy.51 = bf16[512,8,8,128]{3,2,1,0:T(8,128)(2,1)} copy(bf16[512,8,8,128]{3,1,2,0:T(8,128)(2,1)} %bitcast.34) | data formatting | bytes 16777216
  426.5 12.2 %copy.38 = bf16[4,8,128,1024]{3,2,0,1:T(8,128)(2,1)} copy(bf16[4,8,128,1024]{2,1,3,0:T(8,128)(2,1)} %bitcast.77) | data formatting | bytes 16777216 | tf_op jit(solution)/shard_map/reshape | solution.py:29
  438.7 10.0 %all-gather.7.cloned.1.call-done = bf16[4,128,4096]{2,1,0:T(8,128)(2,1)} async-done(((bf16[4,128,1024]{2,1,0:T(8,128)(2,1)}), bf16[4,128,4096]{2,1,0:T(8,128)(2,1)}) %all-gather.7.cloned.1.call-update) | async-done | bytes 4194320 | tf_op jit(solution)/shard_map/all_gather | solution.py:92
  448.7 3.2 fusion
  451.9 0.2 copy-done.1
  452.2 1.5 fusion.1
  453.7 3.4 copy-done.2
  457.1 4.5 convolution_convert_fusion.2
  461.9 0.3 copy-done.11
  462.3 1.4 multiply_reduce_fusion.7
  463.7 0.6 multiply_convert_fusion.3
  464.3 1.0 fusion.75
  465.3 1.0 fusion.74
  466.3 1.0 fusion.73
  467.2 1.0 fusion.72
  468.2 0.3 reduce-scatter.5.cloned.1.call-start
  468.5 10.2 %convolution_convert_fusion.1 = bf16[512,1024]{1,0:T(8,128)(2,1)} fusion(bf16[512,4096]{1,0:T(8,128)(2,1)} %bitcast.86, bf16[4096,1024]{1,0:T(8,128)(2,1)} %bitcast.83), kind=kOutput, calls=%fused_computation.53 | convolution fusion | flops 4295491584 | bytes 13631488 | tf_op jit(solution)/shard_map/dot_general | solution.py:104
  478.7 35.9 %all-reduce.3.cloned.1.call-done = (f32[128,288]{0,1:T(8,128)}, f32[128,288]{0,1:T(8,128)}, f32[128,288]{0,1:T(8,128)}, f32[128,288]{0,1:T(8,128)}) async-done(((f32[128,288]{0,1:T(8,128)}, f32[128,288]{0,1:T(8,128)}, f32[128,288]{0,1:T(8,128)}, f32[128,288]{0,1:T(8,128)}), (f32[128,288]{0,1:T(8,128)}, f32[128,288]{0,1:T(8,128)}, f32[128,288]{0,1:T(8,128)}, ...) | async-done | bytes 589840 | tf_op jit(solution)/shard_map/psum | solution.py:120
  514.6 0.8 fusion.68
  515.4 2.5 convert_multiply_fusion.15
  517.9 2.4 convert_multiply_fusion.9
  520.4 2.4 convert_multiply_fusion.12
  522.8 0.7 fusion.70
  523.5 1.5 convert_multiply_fusion.6
  525.0 0.1 copy.42
  525.1 0.1 copy.43
  525.2 0.1 copy.40
  525.4 0.1 copy.44
  525.5 0.1 copy.39
  525.6 0.1 copy.47
  525.7 0.1 copy.46
  525.8 16.7 %multiply_reduce_fusion.2 = (f32[128,1024]{1,0:T(8,128)S(1)}, f32[128,1024]{1,0:T(8,128)S(1)}, f32[128,1024]{1,0:T(8,128)S(1)}, f32[128,1024]{1,0:T(8,128)S(1)}, f32[128,16,1024]{2,1,0:T(8,128)}) fusion(f32[128,16]{1,0:T(8,128)S(1)} %copy.42, f32[128,16]{1,0:T(8,128)S(1)} %copy.43, f32[128,1024]{1,0:T(8,128)} %get-tuple-element.57, f32[128,16]{1,0:T(8,128)S(1)} %copy.40, ...), kind=kLoop, calls=%fused_computation.10 | loop fusion | flops 49807360 | bytes 23199744 | tf_op jit(solution)/shard_map/reduce_sum | solution.py:133
  542.6 0.8 fusion.60
  543.4 6.2 %convolution_convert_fusion = bf16[4,128,4096]{2,1,0:T(8,128)(2,1)} fusion(bf16[4096,1024,1]{1,0,2:T(8,128)(2,1)S(1)} %bitcast.80, bf16[1,128,1024]{2,1,0:T(8,128)(2,1)S(1)} %get-tuple-element.36, bf16[1,128,1024]{2,1,0:T(8,128)(2,1)S(1)} %get-tuple-element.37, bf16[1,128,1024]{2,1,0:T(8,128)(2,1)S(1)} %get-tuple-element.38, ...), kind=kOutput, calls=%fused_computation.16 | convolution fusion | flops 4298637312 | bytes 13631488 | tf_op jit(solution)/shard_map/dot_general | solution.py:138
  549.7 7.3 %copy.49 = f32[128,2,4096]{2,1,0:T(2,128)} copy(f32[128,2,4096]{0,2,1:T(8,128)} %get-tuple-element.24) | data formatting | bytes 8388608
  557.0 0.9 fusion.29
  558.0 44.5 %reduce-scatter.5.cloned.1.call-done = bf16[4,128,1024]{2,1,0:T(8,128)(2,1)} async-done(((bf16[4,128,4096]{2,1,0:T(8,128)(2,1)}), bf16[4,128,1024]{2,1,0:T(8,128)(2,1)}) %reduce-scatter.5.cloned.1.call-update) | async-done | bytes 1048592 | tf_op jit(solution)/shard_map/reduce_scatter | solution.py:141
  602.4 2.6 add_convert_fusion
  (54 shorter events, 0.9 us)
Async XLA Ops:
  7.2 457.1 %copy-start = (bf16[288,1024]{1,0:T(8,128)(2,1)S(1)}, bf16[288,1024]{1,0:T(8,128)(2,1)}, u32[]{:S(2)}) copy-start(bf16[288,1024]{1,0:T(8,128)(2,1)} %param.33) | copy-start | bytes 1769476
  7.2 96.2 %all-gather.9.cloned.1.call-start = ((), (), s32[]{:S(2)}) async-start(), calls=%async_computation.7 | async-start | bytes 9437184 | tf_op jit(solution)/shard_map/all_gather | solution.py:66
  13.8 167.6 %all-gather.13.cloned.1.call-start = ((), (), s32[]{:S(2)}) async-start(), calls=%async_computation.10 | async-start | bytes 9437184 | tf_op jit(solution)/shard_map/all_gather | solution.py:65
  48.6 2.3 copy-start.14
  50.1 214.2 %all-gather.11.cloned.1.call-start = ((), (), s32[]{:S(2)}) async-start(), calls=%async_computation.9 | async-start | bytes 9437184 | tf_op jit(solution)/shard_map/all_gather | solution.py:64
  50.8 303.4 %reduce-scatter.3.cloned.1.call-start = ((), (), s32[]{:S(2)}) async-start(), calls=%async_computation.5 | async-start | bytes 9437184 | tf_op jit(solution)/shard_map/reduce_scatter | solution.py:88
  111.7 98.8 %all-to-all-start.2 = ((bf16[4,1024,1024]{2,1,0:T(8,128)(2,1)}), bf16[4,1024,1024]{2,1,0:T(8,128)(2,1)}, u32[]{:S(2)}, u32[]{:S(2)}) async-start(bf16[4,1024,1024]{2,1,0:T(8,128)(2,1)} %pad_maximum_fusion), calls=%async_computation.3 | async-start | bytes 16777216 | tf_op jit(solution)/shard_map/all_to_all | solution.py:72
  210.5 98.0 %all-to-all-start.1 = ((bf16[1024,4,1024]{0,2,1:T(8,128)(2,1)}), bf16[1024,4,1024]{0,2,1:T(8,128)(2,1)}, u32[]{:S(2)}, u32[]{:S(2)}) async-start(bf16[1024,4,1024]{0,2,1:T(8,128)(2,1)} %bitcast.82), calls=%async_computation.2 | async-start | bytes 16777216 | tf_op jit(solution)/shard_map/all_to_all | solution.py:70
  308.5 45.9 %copy-start.10 = (f32[16,1024]{1,0:T(8,128)S(1)}, f32[16,1024]{1,0:T(8,128)}, u32[]{:S(2)}) copy-start(f32[16,1024]{1,0:T(8,128)} %param.36) | copy-start | bytes 196612
  308.5 109.0 %all-to-all-start = ((bf16[1024,4,1024]{0,2,1:T(8,128)(2,1)}), bf16[1024,4,1024]{0,2,1:T(8,128)(2,1)}, u32[]{:S(2)}, u32[]{:S(2)}) async-start(bf16[1024,4,1024]{0,2,1:T(8,128)(2,1)} %bitcast.81), calls=%async_computation.1 | async-start | bytes 16777216 | tf_op jit(solution)/shard_map/all_to_all | solution.py:69
  314.4 134.3 %all-gather.7.cloned.1.call-start = ((), (), s32[]{:S(2)}) async-start(), calls=%async_computation.6 | async-start | bytes 5242880 | tf_op jit(solution)/shard_map/all_gather | solution.py:92
  354.2 160.4 %all-reduce.3.cloned.1.call-start = ((), (), s32[]{:S(2)}) async-start(), calls=%async_computation.11 | async-start | bytes 1179648 | tf_op jit(solution)/shard_map/psum | solution.py:120
  448.7 3.4 copy-start.1
  452.2 4.9 copy-start.2
  453.6 7.9 %copy-start.4 = (bf16[4,128,4096]{2,1,0:T(8,128)(2,1)}, bf16[4,128,4096]{2,1,0:T(8,128)(2,1)S(1)}, u32[]{:S(2)}) copy-start(bf16[4,128,4096]{2,1,0:T(8,128)(2,1)S(1)} %fusion.1) | copy-start | bytes 12582916
  457.0 4.6 copy-start.6
  461.6 0.7 copy-start.11
  461.9 1.8 copy-start.12
  468.2 134.2 %reduce-scatter.5.cloned.1.call-start = ((), (), s32[]{:S(2)}) async-start(), calls=%async_computation.8 | async-start | bytes 5242880 | tf_op jit(solution)/shard_map/reduce_scatter | solution.py:141
  468.5 46.9 %copy-start.3 = (bf16[1024,256]{1,0:T(8,128)(2,1)S(1)}, bf16[1024,256]{1,0:T(8,128)(2,1)}, u32[]{:S(2)}) copy-start(bf16[1024,256]{1,0:T(8,128)(2,1)} %param.34) | copy-start | bytes 1572868
  468.5 46.9 %copy-start.9 = (f32[1024]{0:T(1024)S(1)}, f32[1024]{0:T(1024)}, u32[]{:S(2)}) copy-start(f32[1024]{0:T(1024)} %param.35) | copy-start | bytes 12292
  514.6 8.1 %copy-start.8 = (f32[128,288]{0,1:T(8,128)S(1)}, f32[128,288]{0,1:T(8,128)}, u32[]{:S(2)}) copy-start(f32[128,288]{0,1:T(8,128)} %get-tuple-element.17) | copy-start | bytes 442372
  525.8 17.6 %slice-start = ((s8[8388608]{0:T(1024)(128)(4,1)}), s8[4194304]{0:T(1024)(128)(4,1)S(1)}, s32[]{:S(2)}) async-start(s8[8388608]{0:T(1024)(128)(4,1)} %bitcast.78), calls=%async_computation.12 | async-start | bytes 8388608
  525.8 16.8 %copy-start.7 = (bf16[512,1024]{1,0:T(8,128)(2,1)S(1)}, bf16[512,1024]{1,0:T(8,128)(2,1)}, u32[]{:S(2)}) copy-start(bf16[512,1024]{1,0:T(8,128)(2,1)} %convolution_convert_fusion.1) | copy-start | bytes 3145732
  525.8 16.8 %copy-start.13 = (f32[1024]{0:T(1024)S(1)}, f32[1024]{0:T(1024)}, u32[]{:S(2)}) copy-start(f32[1024]{0:T(1024)} %param.37) | copy-start | bytes 12292
  525.8 17.6 %slice-start.1 = ((s8[8388608]{0:T(1024)(128)(4,1)}), s8[4194304]{0:T(1024)(128)(4,1)S(1)}, s32[]{:S(2)}) async-start(s8[8388608]{0:T(1024)(128)(4,1)} %bitcast.78), calls=%async_computation.13 | async-start | bytes 8388608
  549.7 52.7 %copy-start.5 = (bf16[4,128,1024]{2,1,0:T(8,128)(2,1)S(1)}, bf16[4,128,1024]{2,1,0:T(8,128)(2,1)}, u32[]{:S(2)}) copy-start(bf16[4,128,1024]{2,1,0:T(8,128)(2,1)} %reduce-scatter.3.cloned.1.call-done) | copy-start | bytes 3145732
Sparse Core Ops, SparseCore 0:
  13.9 84.8 all-gather.8
  100.4 80.9 all-gather.12
  183.6 80.6 all-gather.10
  266.4 87.6 reduce-scatter.2
  355.9 92.7 all-gather.6
  468.3 46.2 all-reduce.2
  549.8 52.5 reduce-scatter.4
